TPU v7x, 32 devices: a whole 2x2x4 slice. The times are simulated.
32 devices in a mesh: dp: 16 (over z, y, core), mp: 2 (over x).
Axes of the slice: x: 2, y: 2, z: 4, core: 2. Of those that a mesh axis runs over, the one named last changes fastest.
Arguments:
- features: bfloat16 [768, 384], P('dp'), may hold values from -100 to 100
- teacher_weight: float32 [384, 131072], P(None, ('dp', 'mp')), may hold values from -250 to 250
- student_weight: float32 [384, 131072], P(None, ('dp', 'mp')), may hold values from -24 to 24
- center: float32 [131072], P(('dp', 'mp')), may hold values from -1 to 1
Outputs:
- blended: float32 [384, 131072], P(None, ('dp', 'mp'))
- new_center: float32 [131072], P(('dp', 'mp'))
- log_targets: float32 [768, 131072], P(None, ('dp', 'mp'))
All inputs are finite; a program needn't handle non-finite values.
Results may differ from a plain program's by a relative error of at most 0.0003.
Values may be sent and summed in bfloat16 or wider, within the bound.
A program may use at most 64 MiB of HBM per device.

v0:
```python
import jax
import jax.numpy as jnp
from jax import lax
from jax.sharding import PartitionSpec as P

ema_momentum = 0.994
center_momentum = 0.9
teacher_temp = 0.07
epsilon = 1e-06


def shards(features, teacher_weight, student_weight, center):
    blended = ema_momentum * teacher_weight + (1.0 - ema_momentum) * student_weight
    col_norm = jnp.sqrt(jnp.sum(blended * blended, axis=0, keepdims=True) + epsilon)
    protos = (blended / col_norm).astype(jnp.bfloat16)
    wide_feats = features.astype(jnp.float32)
    row_norm = jnp.sqrt(jnp.sum(wide_feats * wide_feats, axis=1, keepdims=True) + epsilon)
    unit_rows = (wide_feats / row_norm).astype(jnp.bfloat16)
    images = features.shape[0] * lax.axis_size("dp")
    logits = jnp.dot(
        lax.all_gather(unit_rows, "dp", axis=0, tiled=True),
        protos,
        preferred_element_type=jnp.float32,
    )
    column_sums = jnp.sum(logits, axis=0)
    new_center = center_momentum * center + (1.0 - center_momentum) * (column_sums / images)
    shifted = (logits - new_center[None, :]) / teacher_temp
    totals = lax.psum(jnp.sum(jnp.exp(shifted), axis=1), ("dp", "mp"))
    log_targets = shifted - jnp.log(totals)[:, None]
    return (blended, new_center, log_targets)


def solution(mesh):
    placed = (P("dp", None), P(None, ("dp", "mp")), P(None, ("dp", "mp")), P(("dp", "mp")))
    return jax.shard_map(
        shards,
        mesh=mesh,
        in_specs=placed,
        out_specs=(P(None, ("dp", "mp")), P(("dp", "mp")), P(None, ("dp", "mp"))),
        check_vma=False,
    )
```

profile of v0, /device:TPU:0, one launch (start us, length us, event | category | flops | bytes accessed | tf_op | source)
XLA Modules:
  0.0 98.3 jit_solution(8793507337813024451)
XLA Ops:
  0.6 0.9 fusion.3
  1.5 0.9 fusion.4
  2.4 24.9 %all_gather.3 = bf16[768,384]{1,0:T(8,128)(2,1)S(1)} all-gather(bf16[48,384]{1,0:T(8,128)(2,1)S(1)} %fusion.4), channel_id=1, replica_groups=mesh['dp'=16,'mp'=2] {'dp'}, dimensions={0}, use_global_device_ids=true | all-gather | bytes 626688 | tf_op jit(solution)/shard_map/all_gather | solution.py:21
  27.3 9.3 %multiply_reduce_fusion = (f32[4096]{0:T(1024)S(1)}, f32[384,4096]{1,0:T(8,128)}) fusion(f32[384,4096]{1,0:T(8,128)} %param.6, f32[384,4096]{1,0:T(8,128)} %param.5), kind=kLoop, calls=%fused_computation.4 | loop fusion | flops 7860224 | bytes 18890752 | tf_op jit(solution)/shard_map/reduce_sum | solution.py:14
  36.6 0.0 copy-start.2
  36.6 5.6 %fusion.5 = (f32[4096]{0:T(1024)S(1)}, f32[768,4096]{1,0:T(8,128)S(1)}) fusion(bf16[768,384]{1,0:T(8,128)(2,1)S(1)} %all_gather.3, f32[384,4096]{1,0:T(8,128)} %get-tuple-element.4, f32[4096]{0:T(1024)S(1)} %add_sqrt_fusion), kind=kOutput, calls=%fused_computation.15 | convolution fusion | flops 2422206464 | bytes 19496960 | tf_op jit(solution)/shard_map/dot_general | solution.py:20
  42.2 0.0 copy-start
  42.2 0.0 copy-done.2
  42.3 4.7 %copy-done = f32[768,4096]{1,0:T(8,128)} copy-done((f32[768,4096]{1,0:T(8,128)}, f32[768,4096]{1,0:T(8,128)S(1)}, u32[]{:S(2)}) %copy-start) | copy-done | bytes 12582936
  47.0 0.0 copy-start.1
  47.0 2.2 %exponential_reduce_fusion = f32[768]{0:T(1024)S(1)} fusion(f32[768,4096]{1,0:T(8,128)S(1)} %get-tuple-element.6, f32[4096]{0:T(1024)S(1)} %multiply_add_fusion.1), kind=kLoop, calls=%fused_computation | loop fusion | flops 9436416 | bytes 12602368 | tf_op jit(solution)/shard_map/reduce_sum | solution.py:28
  49.2 36.9 %psum.7 = f32[768]{0:T(1024)S(1)} all-reduce(f32[768]{0:T(1024)S(1)} %exponential_reduce_fusion), channel_id=1, replica_groups=mesh['dp'=16,'mp'=2] {'dp','mp'}, use_global_device_ids=true, to_apply=%region_4.0 | all-reduce | flops 768 | bytes 6144 | tf_op jit(solution)/shard_map/psum | solution.py:28
  86.0 0.0 copy-done.1
  86.1 12.2 %fusion = f32[768,4096]{1,0:T(8,128)} fusion(f32[768,4096]{1,0:T(8,128)} %copy-done, f32[768]{0:T(1024)S(1)} %log.3, f32[4096]{0:T(1024)S(1)} %multiply_add_fusion.1), kind=kLoop, calls=%fused_computation.2 | loop fusion | flops 9437184 | bytes 25185280 | tf_op jit(solution)/shard_map/sub | solution.py:29
  (4 shorter events, 0.0 us)
Async XLA Ops:
  36.6 5.6 %copy-start.2 = (f32[4096]{0:T(1024)S(1)}, f32[4096]{0:T(1024)}, u32[]{:S(2)}) copy-start(f32[4096]{0:T(1024)} %param.7) | copy-start | bytes 49156
  42.2 4.8 %copy-start = (f32[768,4096]{1,0:T(8,128)}, f32[768,4096]{1,0:T(8,128)S(1)}, u32[]{:S(2)}) copy-start(f32[768,4096]{1,0:T(8,128)S(1)} %get-tuple-element.6) | copy-start | bytes 37748740
  47.0 39.1 %copy-start.1 = (f32[4096]{0:T(1024)}, f32[4096]{0:T(1024)S(1)}, u32[]{:S(2)}) copy-start(f32[4096]{0:T(1024)S(1)} %multiply_add_fusion.1) | copy-start | bytes 49156
where the time goes:
time: 99.2 us; the launch traced here: 98.3 us
  blocking collectives  61.7 us (62%)
  other arithmetic  25.5 us (26%)
  matrix products  5.6 us (6%)
  local copies, waits for them, and re-layouts  4.76 us (5%)
    psum x1, blocking collectives, shards(): totals = lax.psum(jnp.sum(jnp.exp(shifted), axis=1), ('dp', 'mp'))  36.9 us
    all_gather x1, blocking collectives, shards(): lax.all_gather(unit_rows, 'dp', axis=0, tiled=True)  24.9 us
    sub x1, other arithmetic, shards(): log_targets = shifted - jnp.log(totals)[:, None]  12.2 us
    reduce_sum x1, other arithmetic, shards(): jnp.sum(blended * blended, axis=0, keepdims=True) + epsilon  9.32 us
    dot_general x1, matrix products, shards(): jnp.dot(lax.all_gather(unit_rows, 'dp', axis=0, tiled=True), protos, pref...  5.6 us
    unnamed x6, local copies, waits for them, and re-layouts  4.76 us
    reduce_sum x1, other arithmetic, shards(): totals = lax.psum(jnp.sum(jnp.exp(shifted), axis=1), ('dp', 'mp'))  2.18 us

commit v1 on v0

v1 whole, which is shorter than its diff:
```python
import functools

import jax
import jax.numpy as jnp
from jax import lax
from jax.experimental import pallas as pl
from jax.experimental.pallas import tpu as pltpu
from jax.sharding import PartitionSpec as P

ema_momentum = 0.994
center_momentum = 0.9
teacher_temp = 0.07
epsilon = 1e-06

MESH = pl.DeviceIdType.MESH
LANES = 128


def targets_kernel(
    n_dp, n_mp, blend_cols, dot_cols,
    feats_ref, teacher_ref, student_ref, center_ref,
    blended_ref, shifted_ref, new_center_ref, logs_ref,
    raw, student, protos, rows_ref, part, mine, others, old_center,
    own_sem, center_sem, teacher_sem, student_sem,
    send_sem, recv_sem, pass_sem, passed_sem, total_send, total_recv,
):
    dp, mp = lax.axis_index("dp"), lax.axis_index("mp")
    me = dp * n_mp + mp
    n = n_dp * n_mp
    per = raw.shape[1]
    depth, cols = blended_ref.shape
    images = shifted_ref.shape[0]
    extra = rows_ref.shape[0] - images

    blends = cols // blend_cols
    loads = []
    for j in range(blends):
        at = pl.ds(j * blend_cols, blend_cols)
        pair = (
            pltpu.make_async_copy(teacher_ref.at[:, at], blended_ref.at[:, at], teacher_sem.at[j]),
            pltpu.make_async_copy(student_ref.at[:, at], student.at[:, at], student_sem.at[j]),
        )
        for copy in pair:
            copy.start()
        loads.append(pair)
    own = pltpu.make_async_copy(feats_ref, raw.at[dp], own_sem)
    own.start()
    centers_in = pltpu.make_async_copy(center_ref, old_center, center_sem)
    centers_in.start()

    barrier = pltpu.get_barrier_semaphore()

    def greet(o, _):
        peer = lax.rem(me + o, n)
        pl.semaphore_signal(barrier, inc=1, device_id=(peer // n_mp, lax.rem(peer, n_mp)), device_id_type=MESH)
        return 0

    lax.fori_loop(1, n, greet, 0)

    def blend(j):
        for copy in loads[j]:
            copy.wait()
        for c in range(j * blend_cols, (j + 1) * blend_cols, LANES):
            at = slice(c, c + LANES)
            mixed = ema_momentum * blended_ref[:, at] + (1.0 - ema_momentum) * student[:, at]
            blended_ref[:, at] = mixed
            squares = jnp.sum(mixed * mixed, axis=0, keepdims=True)
            protos[:, at] = (mixed * (1.0 / jnp.sqrt(squares + epsilon))).astype(jnp.bfloat16)

    early = min(blends, max(1, blends // 2))
    for j in range(early):
        blend(j)

    pl.semaphore_wait(barrier, n - 1)
    chips = n_dp // 2
    chip, core = dp // 2, lax.rem(dp, 2)
    mate = 2 * chip + 1 - core

    def to_chip(o):
        return pltpu.make_async_remote_copy(
            src_ref=feats_ref,
            dst_ref=raw.at[dp],
            send_sem=send_sem.at[o],
            recv_sem=recv_sem.at[o],
            device_id=(2 * lax.rem(chip + o, chips) + core, mp),
            device_id_type=MESH,
        )

    def source(o):
        return 2 * lax.rem(chip + chips - o, chips) + core

    def to_mate(o):
        src = source(o)
        return pltpu.make_async_remote_copy(
            src_ref=raw.at[src],
            dst_ref=raw.at[src],
            send_sem=pass_sem.at[o],
            recv_sem=passed_sem.at[o],
            device_id=(mate, mp),
            device_id_type=MESH,
        )

    def send(o, _):
        to_chip(o).start()
        return 0

    lax.fori_loop(1, chips, send, 0)

    for j in range(early, blends):
        blend(j)

    def unit(piece, total):
        wide = raw[piece].astype(jnp.float32)
        norm = jnp.sqrt(jnp.sum(wide * wide, axis=1, keepdims=True) + epsilon)
        rows = (wide / norm).astype(jnp.bfloat16)
        rows_ref[pl.ds(pl.multiple_of(extra + piece * per, 16), per), :] = rows
        return total + jnp.sum(rows.astype(jnp.float32), axis=0, keepdims=True)

    own.wait()
    centers_in.wait()
    to_mate(0).start()
    total = unit(dp, jnp.zeros((1, depth), jnp.float32))

    def relay(o, total):
        to_chip(o).wait_recv()
        to_mate(o).start()
        return unit(source(o), total)

    total = lax.fori_loop(1, chips, relay, total)

    def passed(o, total):
        to_mate(o).wait_recv()
        return unit(source(o) + 1 - 2 * core, total)

    total = lax.fori_loop(0, chips, passed, total)

    high = total.astype(jnp.bfloat16).astype(jnp.float32)
    middle = (total - high).astype(jnp.bfloat16).astype(jnp.float32)
    low = total - high - middle
    row = lax.broadcasted_iota(jnp.int32, (extra, depth), 0)
    pieces = jnp.where(row == 0, high, jnp.where(row == 1, middle, jnp.where(row == 2, low, 0.0)))
    rows_ref[0:extra, :] = pieces.astype(jnp.bfloat16)

    part[...] = jnp.zeros_like(part)
    block = 64

    def targets(j, _):
        start = pl.multiple_of(j * dot_cols, dot_cols)
        logits = jnp.dot(rows_ref[...], protos[:, pl.ds(start, dot_cols)], preferred_element_type=jnp.float32)
        centers = []
        for t in range(dot_cols // LANES):
            sums = jnp.sum(logits[0:8, t * LANES:(t + 1) * LANES], axis=0, keepdims=True)
            spot = pl.ds(j * (dot_cols // LANES) + t, 1)
            fresh = center_momentum * old_center[spot, :] + (1.0 - center_momentum) * (sums / images)
            new_center_ref[spot, :] = fresh
            centers.append(fresh)
        for r in range(0, images, block):
            acc = part[r:r + block, :]
            for t, fresh in enumerate(centers):
                logit = logits[extra + r:extra + r + block, t * LANES:(t + 1) * LANES]
                shifted = (logit - fresh) * (1.0 / teacher_temp)
                shifted_ref[r:r + block, pl.ds(pl.multiple_of(start + t * LANES, LANES), LANES)] = shifted
                acc = acc + jnp.exp(shifted)
            part[r:r + block, :] = acc
        return 0

    lax.fori_loop(0, cols // dot_cols, targets, 0, unroll=2 if cols // dot_cols % 2 == 0 else 1)

    mine[...] = jnp.ones_like(mine)
    for i in range(images // LANES):
        mine[i:i + 1, :] = jnp.sum(part[i * LANES:(i + 1) * LANES, :].T, axis=0, keepdims=True)

    def share(o, _):
        peer = lax.rem(me + o, n)
        pltpu.make_async_remote_copy(
            src_ref=mine,
            dst_ref=others.at[o - 1],
            send_sem=total_send,
            recv_sem=total_recv,
            device_id=(peer // n_mp, lax.rem(peer, n_mp)),
            device_id_type=MESH,
        ).start()
        return 0

    lax.fori_loop(1, n, share, 0)

    def sent(o, _):
        to_chip(o).wait_send()
        return 0

    lax.fori_loop(1, chips, sent, 0)

    def handed(o, _):
        to_mate(o).wait_send()
        return 0

    lax.fori_loop(0, chips, handed, 0)

    pltpu.make_async_copy(others, others, total_recv).wait()
    logs = jnp.log(mine[...] + jnp.sum(others[...], axis=0))
    for i in range(images // LANES):
        logs_ref[i * LANES:(i + 1) * LANES, :] = jnp.broadcast_to(logs[i:i + 1, :], (LANES, LANES)).T
    pltpu.make_async_copy(others, others, total_send).wait()


def finish_kernel(
    chunks, blended_in, shifted_ref, center_in, logs_ref,
    blended_out, center_out, out_ref, stage, blended_sem, center_sem, out_sem,
):
    images, cols = shifted_ref.shape
    step = images // chunks
    center = pltpu.make_async_copy(center_in, center_out, center_sem)
    blended = pltpu.make_async_copy(blended_in, blended_out, blended_sem)
    waits = [center, blended]
    center.start()
    blended.start()
    for i in range(chunks):
        log = logs_ref[i * step:(i + 1) * step, :]
        for c in range(0, cols, LANES):
            stage[i * step:(i + 1) * step, c:c + LANES] = shifted_ref[i * step:(i + 1) * step, c:c + LANES] - log
        at = pl.ds(i * step, step)
        copy = pltpu.make_async_copy(stage.at[at, :], out_ref.at[at, :], out_sem.at[i])
        copy.start()
        waits.append(copy)
    for copy in waits:
        copy.wait()


def solution(mesh):
    n_dp, n_mp = mesh.shape["dp"], mesh.shape["mp"]
    n = n_dp * n_mp

    def shards(features, teacher_weight, student_weight, center):
        per, depth = features.shape
        cols = teacher_weight.shape[1]
        images = per * n_dp
        tiles = cols // LANES
        blend_cols = min(cols, 512)
        dot_cols = min(cols, 512)
        held = -(-images // (8 * LANES)) * 8
        f32 = jnp.float32
        whole = pl.BlockSpec(memory_space=pltpu.VMEM)
        far = pl.BlockSpec(memory_space=pl.ANY)
        near = pl.BlockSpec(memory_space=pltpu.HBM)
        dma = pltpu.SemaphoreType.DMA
        blended, shifted, new_center, logs = pl.pallas_call(
            functools.partial(targets_kernel, n_dp, n_mp, blend_cols, dot_cols),
            out_shape=(
                pltpu.VMEM((depth, cols), f32),
                pltpu.VMEM((images, cols), f32),
                pltpu.VMEM((tiles, LANES), f32),
                pltpu.VMEM((images, LANES), f32),
            ),
            in_specs=[near] * 4,
            out_specs=(whole, whole, whole, whole),
            scratch_shapes=[
                pltpu.VMEM((n_dp, per, depth), jnp.bfloat16),
                pltpu.VMEM((depth, cols), f32),
                pltpu.VMEM((depth, cols), jnp.bfloat16),
                pltpu.VMEM((16 + images, depth), jnp.bfloat16),
                pltpu.VMEM((images, LANES), f32),
                pltpu.VMEM((held, LANES), f32),
                pltpu.VMEM((n - 1, held, LANES), f32),
                pltpu.VMEM((tiles, LANES), f32),
                dma, dma, dma((cols // blend_cols,)), dma((cols // blend_cols,)),
                dma((n_dp // 2,)), dma((n_dp // 2,)), dma((n_dp // 2,)), dma((n_dp // 2,)),
                dma, dma,
            ],
            compiler_params=pltpu.CompilerParams(
                collective_id=0, has_side_effects=True, vmem_limit_bytes=20 * 2**20
            ),
            name="targets",
        )(features, teacher_weight, student_weight, center.reshape(tiles, LANES))
        chunks = 16
        blended, new_center, log_targets = pl.pallas_call(
            functools.partial(finish_kernel, chunks),
            out_shape=(
                jax.ShapeDtypeStruct((depth, cols), f32),
                jax.ShapeDtypeStruct((tiles, LANES), f32),
                jax.ShapeDtypeStruct((images, cols), f32),
            ),
            in_specs=[whole] * 4,
            out_specs=(far, far, far),
            scratch_shapes=[pltpu.VMEM((images, cols), f32), dma, dma, dma((chunks,))],
            compiler_params=pltpu.CompilerParams(vmem_limit_bytes=16 * 2**20),
            name="finish",
        )(blended, shifted, new_center, logs)
        return blended, new_center.reshape(cols), log_targets

    placed = (P("dp", None), P(None, ("dp", "mp")), P(None, ("dp", "mp")), P(("dp", "mp")))
    return jax.shard_map(
        shards,
        mesh=mesh,
        in_specs=placed,
        out_specs=(P(None, ("dp", "mp")), P(("dp", "mp")), P(None, ("dp", "mp"))),
        check_vma=False,
    )
```

time: 99.2 us -> 43.2 us (0.44)
  blocking collectives: 61.7 us -> 0 us
  Pallas kernels: 0 us -> 35.2 us
  other arithmetic: 25.5 us -> 0 us
  matrix products: 5.6 us -> 0 us
  local copies, waits for them, and re-layouts: 4.76 us -> 7.05 us
    psum x1 -> x0, blocking collectives: 36.9 us -> none  [shards(): totals = lax.psum(jnp.sum(jnp.exp(shifted), axis=1), ('dp', 'mp'))]
    pallas_call x0 -> x2, Pallas kernels: none -> 35.2 us  [the longest x1 28.5 us: shards(): pl.pallas_call(functools.partial(targets_kernel, n_dp, n_mp, blend_cols,...]
    all_gather x1 -> x0, blocking collectives: 24.9 us -> none  [shards(): lax.all_gather(unit_rows, 'dp', axis=0, tiled=True)]
    reduce_sum x3 -> x0, other arithmetic: 12.4 us -> none  [the longest x1 9.32 us: shards(): jnp.sum(blended * blended, axis=0, keepdims=True) + epsilon]
    sub x1 -> x0, other arithmetic: 12.2 us -> none  [shards(): log_targets = shifted - jnp.log(totals)[:, None]]
    dot_general x1 -> x0, matrix products: 5.6 us -> none  [shards(): jnp.dot(lax.all_gather(unit_rows, 'dp', axis=0, tiled=True), protos, pref...]
    unnamed x6 -> x8, local copies, waits for them, and re-layouts: 4.76 us -> 7.05 us
where the time goes in v1:
time: 43.2 us; the launch traced here: 42.9 us
  Pallas kernels  35.2 us (81%)
  local copies, waits for them, and re-layouts  7.05 us (16%)
  between operations  0.65 us (2%)
    pallas_call x1, Pallas kernels, shards(): pl.pallas_call(functools.partial(targets_kernel, n_dp, n_mp, blend_cols,...  28.5 us
    unnamed x8, local copies, waits for them, and re-layouts  7.05 us
    pallas_call x1, Pallas kernels, shards(): pl.pallas_call(functools.partial(finish_kernel, chunks), out_shape=(jax.S...  6.67 us

profile of v1, /device:TPU:0, one launch (start us, length us, event | category | flops | bytes accessed | tf_op | source)
XLA Modules:
  0.0 42.9 jit_solution(13501809709733713331)
XLA Ops:
  0.6 0.0 copy-start
  0.6 2.8 %copy-done = f32[384,4096]{1,0:T(8,128)S(1)} copy-done((f32[384,4096]{1,0:T(8,128)S(1)}, f32[384,4096]{1,0:T(8,128)}, u32[]{:S(2)}) %copy-start) | copy-done | bytes 6291480
  3.4 0.0 copy-start.1
  3.4 2.8 %copy-done.1 = f32[384,4096]{1,0:T(8,128)S(1)} copy-done((f32[384,4096]{1,0:T(8,128)S(1)}, f32[384,4096]{1,0:T(8,128)}, u32[]{:S(2)}) %copy-start.1) | copy-done | bytes 6291480
  6.2 0.0 copy-start.2
  6.2 0.8 %copy-done.2 = bf16[48,384]{1,0:T(8,128)(2,1)S(1)} copy-done((bf16[48,384]{1,0:T(8,128)(2,1)S(1)}, bf16[48,384]{1,0:T(8,128)(2,1)}, u32[]{:S(2)}) %copy-start.2) | copy-done | bytes 36888
  7.0 0.0 copy-start.3
  7.0 0.7 %copy-done.3 = f32[4096]{0:T(1024)S(1)} copy-done((f32[4096]{0:T(1024)S(1)}, f32[4096]{0:T(1024)}, u32[]{:S(2)}) %copy-start.3) | copy-done | bytes 16408
  7.7 28.5 %targets.1 = (f32[384,4096]{1,0:T(8,128)S(1)}, f32[768,4096]{1,0:T(8,128)S(1)}, f32[32,128]{1,0:T(8,128)S(1)}, f32[768,128]{1,0:T(8,128)S(1)}) custom-call(bf16[48,384]{1,0:T(8,128)(2,1)S(1)} %copy-done.2, f32[384,4096]{1,0:T(8,128)S(1)} %copy-done, f32[384,4096]{1,0:T(8,128)S(1)} %copy-done.1, f32[32,128]{1,0:T(8,128)S(1)} %bitcast.2), custom_call_target="tpu_custom_call" | custom-call | tf_op jit(solution)/shard_map/targets/pallas_call | solution.py:246
  36.2 6.7 %finish.1 = (f32[384,4096]{1,0:T(8,128)}, f32[32,128]{1,0:T(8,128)}, f32[768,4096]{1,0:T(8,128)}) custom-call(f32[384,4096]{1,0:T(8,128)S(1)} %get-tuple-element.10.blended_in, f32[768,4096]{1,0:T(8,128)S(1)} %get-tuple-element.11.shifted_ref, f32[32,128]{1,0:T(8,128)S(1)} %get-tuple-element.12.center_in, f32[768,128]{1,0:T(8,128)S(1)} %get-tuple-element.13.logs_ref), custom_call_target="tpu_custom_call" | custom-call | tf_op jit(solution)/shard_map/finish/pallas_call | solution.py:275
Async XLA Ops:
  0.6 2.8 %copy-start = (f32[384,4096]{1,0:T(8,128)S(1)}, f32[384,4096]{1,0:T(8,128)}, u32[]{:S(2)}) copy-start(f32[384,4096]{1,0:T(8,128)} %teacher_ref.1) | copy-start | bytes 18874372
  3.4 2.8 %copy-start.1 = (f32[384,4096]{1,0:T(8,128)S(1)}, f32[384,4096]{1,0:T(8,128)}, u32[]{:S(2)}) copy-start(f32[384,4096]{1,0:T(8,128)} %student_ref.1) | copy-start | bytes 18874372
  6.2 0.8 %copy-start.2 = (bf16[48,384]{1,0:T(8,128)(2,1)S(1)}, bf16[48,384]{1,0:T(8,128)(2,1)}, u32[]{:S(2)}) copy-start(bf16[48,384]{1,0:T(8,128)(2,1)} %feats_ref.1) | copy-start | bytes 110596
  7.0 0.7 %copy-start.3 = (f32[4096]{0:T(1024)S(1)}, f32[4096]{0:T(1024)}, u32[]{:S(2)}) copy-start(f32[4096]{0:T(1024)} %param.7) | copy-start | bytes 49156

commit v2 on v1

--- a/solution.py
+++ b/solution.py
@@ -25,9 +25,8 @@
     send_sem, recv_sem, pass_sem, passed_sem, total_send, total_recv,
 ):
     dp, mp = lax.axis_index("dp"), lax.axis_index("mp")
-    me = dp * n_mp + mp
     n = n_dp * n_mp
-    per = raw.shape[1]
+    per = raw.shape[2]
     depth, cols = blended_ref.shape
     images = shifted_ref.shape[0]
     extra = rows_ref.shape[0] - images
@@ -43,19 +42,73 @@
         for copy in pair:
             copy.start()
         loads.append(pair)
-    own = pltpu.make_async_copy(feats_ref, raw.at[dp], own_sem)
+    own = pltpu.make_async_copy(feats_ref, raw.at[lax.rem(dp, 2), dp // 2], own_sem)
     own.start()
     centers_in = pltpu.make_async_copy(center_ref, old_center, center_sem)
     centers_in.start()
 
     barrier = pltpu.get_barrier_semaphore()
 
-    def greet(o, _):
-        peer = lax.rem(me + o, n)
-        pl.semaphore_signal(barrier, inc=1, device_id=(peer // n_mp, lax.rem(peer, n_mp)), device_id_type=MESH)
-        return 0
-
-    lax.fori_loop(1, n, greet, 0)
+    rings = n_dp // 4
+    outer, inner, core = dp // 4, lax.rem(dp // 2, 2), lax.rem(dp, 2)
+    mate = dp + 1 - 2 * core
+    beside = dp + 2 - 4 * inner
+
+    def each_peer(act):
+        for b in range(1, n_mp):
+            act(b - 1, dp, lax.rem(mp + b, n_mp))
+
+        def row(a, _):
+            there = lax.rem(dp + a, n_dp)
+            for b in range(n_mp):
+                act(a * n_mp + b - 1, there, lax.rem(mp + b, n_mp))
+            return 0
+
+        lax.fori_loop(1, n_dp, row, 0, unroll=n_dp <= 16)
+
+    each_peer(lambda slot, d, m: pl.semaphore_signal(barrier, inc=1, device_id=(d, m), device_id_type=MESH))
+
+    def place(o, f):
+        near = inner + f * (1 - 2 * inner)
+        return 2 * lax.rem(outer + rings - o, rings) + near
+
+    def around(o):
+        return pltpu.make_async_remote_copy(
+            src_ref=feats_ref,
+            dst_ref=raw.at[core, dp // 2],
+            send_sem=send_sem.at[o],
+            recv_sem=recv_sem.at[o],
+            device_id=(4 * lax.rem(outer + o, rings) + 2 * inner + core, mp),
+            device_id_type=MESH,
+        )
+
+    def across(o):
+        spot = raw.at[core, place(o, 0)]
+        return pltpu.make_async_remote_copy(
+            src_ref=feats_ref if o == 0 else spot,
+            dst_ref=spot,
+            send_sem=send_sem.at[rings + o],
+            recv_sem=recv_sem.at[rings + o],
+            device_id=(beside, mp),
+            device_id_type=MESH,
+        )
+
+    def to_mate(o, f):
+        spot = raw.at[core, place(o, f)]
+        return pltpu.make_async_remote_copy(
+            src_ref=feats_ref if o == 0 and f == 0 else spot,
+            dst_ref=spot,
+            send_sem=pass_sem.at[f * rings + o],
+            recv_sem=passed_sem.at[f * rings + o],
+            device_id=(mate, mp),
+            device_id_type=MESH,
+        )
+
+    pl.semaphore_wait(barrier, n - 1)
+    for o in sorted(range(1, rings), key=lambda o: -min(o, rings - o)):
+        around(o).start()
+    across(0).start()
+    to_mate(0, 0).start()
 
     def blend(j):
         for copy in loads[j]:
@@ -67,72 +120,31 @@
             squares = jnp.sum(mixed * mixed, axis=0, keepdims=True)
             protos[:, at] = (mixed * (1.0 / jnp.sqrt(squares + epsilon))).astype(jnp.bfloat16)
 
-    early = min(blends, max(1, blends // 2))
-    for j in range(early):
+    for j in range(blends):
         blend(j)
 
-    pl.semaphore_wait(barrier, n - 1)
-    chips = n_dp // 2
-    chip, core = dp // 2, lax.rem(dp, 2)
-    mate = 2 * chip + 1 - core
-
-    def to_chip(o):
-        return pltpu.make_async_remote_copy(
-            src_ref=feats_ref,
-            dst_ref=raw.at[dp],
-            send_sem=send_sem.at[o],
-            recv_sem=recv_sem.at[o],
-            device_id=(2 * lax.rem(chip + o, chips) + core, mp),
-            device_id_type=MESH,
-        )
-
-    def source(o):
-        return 2 * lax.rem(chip + chips - o, chips) + core
-
-    def to_mate(o):
-        src = source(o)
-        return pltpu.make_async_remote_copy(
-            src_ref=raw.at[src],
-            dst_ref=raw.at[src],
-            send_sem=pass_sem.at[o],
-            recv_sem=passed_sem.at[o],
-            device_id=(mate, mp),
-            device_id_type=MESH,
-        )
-
-    def send(o, _):
-        to_chip(o).start()
-        return 0
-
-    lax.fori_loop(1, chips, send, 0)
-
-    for j in range(early, blends):
-        blend(j)
-
-    def unit(piece, total):
-        wide = raw[piece].astype(jnp.float32)
-        norm = jnp.sqrt(jnp.sum(wide * wide, axis=1, keepdims=True) + epsilon)
+    def unit(half):
+        wide = raw[half].astype(jnp.float32)
+        norm = jnp.sqrt(jnp.sum(wide * wide, axis=2, keepdims=True) + epsilon)
         rows = (wide / norm).astype(jnp.bfloat16)
-        rows_ref[pl.ds(pl.multiple_of(extra + piece * per, 16), per), :] = rows
-        return total + jnp.sum(rows.astype(jnp.float32), axis=0, keepdims=True)
+        for c in range(n_dp // 2):
+            rows_ref[pl.ds(pl.multiple_of(extra + (2 * c + half) * per, 16), per), :] = rows[c]
+        return jnp.sum(jnp.sum(rows.astype(jnp.float32), axis=0), axis=0, keepdims=True)
 
     own.wait()
     centers_in.wait()
-    to_mate(0).start()
-    total = unit(dp, jnp.zeros((1, depth), jnp.float32))
-
-    def relay(o, total):
-        to_chip(o).wait_recv()
-        to_mate(o).start()
-        return unit(source(o), total)
-
-    total = lax.fori_loop(1, chips, relay, total)
-
-    def passed(o, total):
-        to_mate(o).wait_recv()
-        return unit(source(o) + 1 - 2 * core, total)
-
-    total = lax.fori_loop(0, chips, passed, total)
+    for o in sorted(range(1, rings), key=lambda o: min(o, rings - o)):
+        around(o).wait_recv()
+        across(o).start()
+        to_mate(o, 0).start()
+    for o in sorted(range(rings), key=lambda o: min(o, rings - o)):
+        across(o).wait_recv()
+        to_mate(o, 1).start()
+    total = unit(core)
+    for f in range(2):
+        for o in range(rings):
+            to_mate(o, f).wait_recv()
+    total = total + unit(1 - core)
 
     high = total.astype(jnp.bfloat16).astype(jnp.float32)
     middle = (total - high).astype(jnp.bfloat16).astype(jnp.float32)
@@ -170,31 +182,24 @@
     for i in range(images // LANES):
         mine[i:i + 1, :] = jnp.sum(part[i * LANES:(i + 1) * LANES, :].T, axis=0, keepdims=True)
 
-    def share(o, _):
-        peer = lax.rem(me + o, n)
+    def share(slot, d, m):
         pltpu.make_async_remote_copy(
             src_ref=mine,
-            dst_ref=others.at[o - 1],
+            dst_ref=others.at[slot],
             send_sem=total_send,
             recv_sem=total_recv,
-            device_id=(peer // n_mp, lax.rem(peer, n_mp)),
+            device_id=(d, m),
             device_id_type=MESH,
         ).start()
-        return 0
-
-    lax.fori_loop(1, n, share, 0)
-
-    def sent(o, _):
-        to_chip(o).wait_send()
-        return 0
-
-    lax.fori_loop(1, chips, sent, 0)
-
-    def handed(o, _):
-        to_mate(o).wait_send()
-        return 0
-
-    lax.fori_loop(0, chips, handed, 0)
+
+    each_peer(share)
+
+    for o in range(rings):
+        if o:
+            around(o).wait_send()
+        across(o).wait_send()
+        for f in range(2):
+            to_mate(o, f).wait_send()
 
     pltpu.make_async_copy(others, others, total_recv).wait()
     logs = jnp.log(mine[...] + jnp.sum(others[...], axis=0))
@@ -240,6 +245,7 @@
         held = -(-images // (8 * LANES)) * 8
         f32 = jnp.float32
         whole = pl.BlockSpec(memory_space=pltpu.VMEM)
+        operands = (features, teacher_weight, student_weight, center.reshape(tiles, LANES))
         far = pl.BlockSpec(memory_space=pl.ANY)
         near = pl.BlockSpec(memory_space=pltpu.HBM)
         dma = pltpu.SemaphoreType.DMA
@@ -254,7 +260,7 @@
             in_specs=[near] * 4,
             out_specs=(whole, whole, whole, whole),
             scratch_shapes=[
-                pltpu.VMEM((n_dp, per, depth), jnp.bfloat16),
+                pltpu.VMEM((2, n_dp // 2, per, depth), jnp.bfloat16),
                 pltpu.VMEM((depth, cols), f32),
                 pltpu.VMEM((depth, cols), jnp.bfloat16),
                 pltpu.VMEM((16 + images, depth), jnp.bfloat16),
@@ -270,7 +276,7 @@
                 collective_id=0, has_side_effects=True, vmem_limit_bytes=20 * 2**20
             ),
             name="targets",
-        )(features, teacher_weight, student_weight, center.reshape(tiles, LANES))
+        )(*(pltpu.with_memory_space_constraint(x, pltpu.HBM) for x in operands))
         chunks = 16
         blended, new_center, log_targets = pl.pallas_call(
             functools.partial(finish_kernel, chunks),

time: 43.2 us -> 34 us (0.79)
  local copies, waits for them, and re-layouts: 7.05 us -> 0 us
  Pallas kernels: 35.2 us -> 33.2 us
    unnamed x8 -> x0, local copies, waits for them, and re-layouts: 7.05 us -> none
    pallas_call x1, Pallas kernels: 28.5 us -> 26.6 us  [shards(): pl.pallas_call(functools.partial(targets_kernel, n_dp, n_mp, blend_cols,...]
where the time goes in v2:
time: 34 us; the launch traced here: 33.9 us
  Pallas kernels  33.2 us (98%)
  between operations  0.64 us (2%)
    pallas_call x1, Pallas kernels, shards(): pl.pallas_call(functools.partial(targets_kernel, n_dp, n_mp, blend_cols,...  26.6 us
    pallas_call x1, Pallas kernels, shards(): pl.pallas_call(functools.partial(finish_kernel, chunks), out_shape=(jax.S...  6.67 us

profile of v2, /device:TPU:0, one launch (start us, length us, event | category | flops | bytes accessed | tf_op | source)
XLA Modules:
  0.0 33.9 jit_solution(9365721228481735101)
XLA Ops:
  0.6 26.6 %targets.1 = (f32[384,4096]{1,0:T(8,128)S(1)}, f32[768,4096]{1,0:T(8,128)S(1)}, f32[32,128]{1,0:T(8,128)S(1)}, f32[768,128]{1,0:T(8,128)S(1)}) custom-call(bf16[48,384]{1,0:T(8,128)(2,1)} %feats_ref.1, f32[384,4096]{1,0:T(8,128)} %teacher_ref.1, f32[384,4096]{1,0:T(8,128)} %student_ref.1, f32[32,128]{1,0:T(8,128)} %bitcast.2), custom_call_target="tpu_custom_call" | custom-call | tf_op jit(solution)/shard_map/targets/pallas_call | solution.py:252
  27.2 6.7 %finish.1 = (f32[384,4096]{1,0:T(8,128)}, f32[32,128]{1,0:T(8,128)}, f32[768,4096]{1,0:T(8,128)}) custom-call(f32[384,4096]{1,0:T(8,128)S(1)} %get-tuple-element.10.blended_in, f32[768,4096]{1,0:T(8,128)S(1)} %get-tuple-element.11.shifted_ref, f32[32,128]{1,0:T(8,128)S(1)} %get-tuple-element.12.center_in, f32[768,128]{1,0:T(8,128)S(1)} %get-tuple-element.13.logs_ref), custom_call_target="tpu_custom_call" | custom-call | tf_op jit(solution)/shard_map/finish/pallas_call | solution.py:281
